TPU v7x, 16 devices: a whole 2x2x2 slice. The times are simulated.
16 devices in a mesh: rows: 16 (over z, y, x, core).
Axes of the slice: x: 2, y: 2, z: 2, core: 2. Of those that a mesh axis runs over, the one named last changes fastest.
Arguments:
- a_mat: float32 [262144, 64], P('rows')
- b_mat: float32 [262144, 4], P('rows')
Outputs:
- output 1: float32 [262144, 64], P('rows')
- output 2: float32 [64, 64], replicated
- output 3: float32 [64, 4], replicated
All inputs are finite; a program needn't handle non-finite values.
Results may differ from a plain program's by a relative error of at most 0.001.
Values sent between devices are 32-bit elements.
A program may use at most 1 GiB of HBM per device.

v0:
```python
import jax
import jax.numpy as jnp
from jax import lax
from jax.sharding import PartitionSpec as P

FULL_PRECISION = lax.Precision.HIGHEST


def solution(mesh):
    def local_fn(a_blk, b_blk):
        rows_local, num_cols = a_blk.shape
        dev_index = lax.axis_index('rows')
        global_row = dev_index * rows_local + jnp.arange(rows_local)
        col_ids = jnp.arange(num_cols)

        def factor_step(col_idx, carry):
            work_mat, reflectors, tau_vec = carry
            column = lax.dynamic_index_in_dim(work_mat, col_idx, axis=1, keepdims=False)
            below_mask = global_row >= col_idx
            at_pivot = global_row == col_idx
            column = jnp.where(below_mask, column, 0.0)
            local_stats = jnp.stack([jnp.sum(column * column), jnp.sum(jnp.where(at_pivot, column, 0.0))])
            col_stats = lax.psum(local_stats, 'rows')
            norm_val = jnp.sqrt(col_stats[0])
            pivot_val = col_stats[1]
            beta_val = jnp.where(pivot_val >= 0.0, -norm_val, norm_val)
            reflector = jnp.where(at_pivot, 1.0, column / (pivot_val - beta_val))
            tau_val = (beta_val - pivot_val) / beta_val
            part_proj = jnp.dot(reflector, work_mat, precision=FULL_PRECISION, preferred_element_type=jnp.float32)
            row_proj = lax.psum(part_proj, 'rows')
            work_mat = work_mat - (tau_val * reflector)[:, None] * row_proj[None, :]
            reflectors = lax.dynamic_update_index_in_dim(reflectors, reflector, col_idx, 0)
            tau_vec = jnp.where(col_ids == col_idx, tau_val, tau_vec)
            return work_mat, reflectors, tau_vec

        init_state = (a_blk, jnp.zeros((num_cols, rows_local), jnp.float32), jnp.zeros((num_cols,), jnp.float32))
        work_mat, reflectors, tau_vec = lax.fori_loop(0, num_cols, factor_step, init_state)
        top_rows = jnp.triu(work_mat[:num_cols])
        r_full = lax.psum(jnp.where(dev_index == 0, top_rows, 0.0), 'rows')

        def form_step(step_idx, q_work):
            col_idx = num_cols - 1 - step_idx
            reflector = lax.dynamic_index_in_dim(reflectors, col_idx, axis=0, keepdims=False)
            tau_val = lax.dynamic_index_in_dim(tau_vec, col_idx, axis=0, keepdims=False)
            part_proj = jnp.dot(reflector, q_work, precision=FULL_PRECISION, preferred_element_type=jnp.float32)
            row_proj = lax.psum(part_proj, 'rows')
            return q_work - (tau_val * reflector)[:, None] * row_proj[None, :]

        eye_part = (global_row[:, None] == col_ids[None, :]).astype(jnp.float32)
        q_work = lax.fori_loop(0, num_cols, form_step, eye_part)
        diag_signs = jnp.sign(jnp.diagonal(r_full))
        q_blk = q_work * diag_signs[None, :]
        r_fac = r_full * diag_signs[:, None]
        part_c = jnp.einsum('rn,rk->nk', q_blk, b_blk, precision=FULL_PRECISION, preferred_element_type=jnp.float32)
        c_mat = lax.psum(part_c, 'rows')
        return q_blk, r_fac, c_mat

    return jax.shard_map(local_fn, mesh=mesh, in_specs=(P('rows', None), P('rows', None)), out_specs=(P('rows', None), P(), P()), check_vma=False)
```

profile of v0, /device:TPU:0, one launch (start us, length us, event | category | flops | bytes accessed | tf_op | source)
XLA Modules:
  0.0 8759.8 jit_solution(16071496546334230302)
XLA Ops:
  5.2 5496.1 %while.34 = (s32[]{:T(128)}, f32[16384,64]{0,1:T(8,128)}, f32[64,16384]{1,0:T(8,128)}, f32[64]{0:T(128)S(1)}, s32[]{:T(128)}, /*index=5*/s32[]{:T(128)}, f32[]{:T(128)}, s32[]{:T(128)}) while((s32[]{:T(128)}, f32[16384,64]{0,1:T(8,128)}, f32[64,16384]{1,0:T(8,128)}, f32[64]{0:T(128)S(1)}, s32[]{:T(128)}, /*index=5*/s32[]{:T(128)}, ...), condition=%wide.region_5.6_spmd.clone, body=%wide.region_0.5_spmd.clone.sunk | while | flops 15073547 | bytes 13535009 | solution.py:37
  8.3 34.6 psum.58
  5510.7 3159.5 %while.33 = (s32[]{:T(128)}, f32[16384,64]{1,0:T(8,128)}, f32[64]{0:T(128)S(1)}, f32[64,16384]{1,0:T(8,128)}, s32[]{:T(128)}, /*index=5*/s32[]{:T(128)}, s32[]{:T(128)}, s32[]{:T(128)}) while((s32[]{:T(128)}, f32[16384,64]{1,0:T(8,128)}, f32[64]{0:T(128)S(1)}, f32[64,16384]{1,0:T(8,128)}, s32[]{:T(128)}, /*index=5*/s32[]{:T(128)}, s32[]{:T(128)}, ...), condition=%wide.region_8.9_spmd, body=%wide.region_6.8_spmd.sunk | while | flops 14696518 | bytes 12977303 | solution.py:50
  5519.5 32.7 psum.57
  5568.9 32.7 psum.57
  5618.2 32.7 psum.57
  5667.6 32.7 psum.57
  5717.0 32.7 psum.57
  5766.3 32.7 psum.57
  5815.7 32.7 psum.57
  5865.1 32.7 psum.57
  5914.5 32.7 psum.57
  5963.8 32.7 psum.57
  6013.2 32.7 psum.57
  6062.6 32.7 psum.57
  6111.9 32.7 psum.57
  6161.3 32.7 psum.57
  6210.7 32.7 psum.57
  6260.0 32.7 psum.57
  6309.4 32.7 psum.57
  6358.8 32.7 psum.57
  6408.1 32.7 psum.57
  6457.5 32.7 psum.57
  6506.9 32.7 psum.57
  6556.2 32.7 psum.57
  6655.0 32.7 psum.57
  6753.7 32.7 psum.57
  6852.4 32.7 psum.57
  6901.8 32.7 psum.57
  7000.5 32.7 psum.57
  7099.3 32.7 psum.57
  7198.0 32.7 psum.57
  7247.4 32.7 psum.57
  7346.1 32.7 psum.57
  7444.8 32.7 psum.57
  7592.9 32.7 psum.57
  7691.7 32.7 psum.57
  7790.4 32.7 psum.57
  7839.8 32.7 psum.57
  7938.5 32.7 psum.57
  8037.2 32.7 psum.57
  8136.0 32.7 psum.57
  8185.4 32.7 psum.57
  8284.1 32.7 psum.57
  8382.8 32.7 psum.57
  8530.9 32.7 psum.57
  8629.7 32.7 psum.57
  8684.8 33.0 psum.50
  (1255 shorter events, 7076.6 us)
Async XLA Ops:
  0.6 8722.5 %copy-start = (f32[16384,4]{0,1:T(4,128)S(1)}, f32[16384,4]{0,1:T(4,128)}, u32[]{:S(2)}) copy-start(f32[16384,4]{0,1:T(4,128)} %param.7) | copy-start | bytes 786436
  8721.1 2.0 copy-start.1
where the time goes:
time: 8800 us; the launch traced here: 8760 us
  blocking collectives  6330 us (72%)
  other arithmetic  1150 us (13%)
  matrix products  740 us (8%)
  local copies, waits for them, and re-layouts  364 us (4%)
  loops' own time  177 us (2%)
    psum x64, blocking collectives, form_step(): row_proj = lax.psum(part_proj, 'rows')  2090 us
    psum x64, blocking collectives, factor_step(): col_stats = lax.psum(local_stats, 'rows')  2090 us
    psum x64, blocking collectives, factor_step(): row_proj = lax.psum(part_proj, 'rows')  2090 us
    sub x64, other arithmetic, form_step(): return q_work - (tau_val * reflector)[:, None] * row_proj[None, :]  505 us
    dot_general x64, matrix products, form_step(): jnp.dot(reflector, q_work, precision=FULL_PRECISION, preferred_element_ty...  413 us
    dot_general x64, matrix products, factor_step(): jnp.dot(reflector, work_mat, precision=FULL_PRECISION, preferred_element_...  324 us
    sub x64, other arithmetic, factor_step(): work_mat = work_mat - (tau_val * reflector)[:, None] * row_proj[None, :]  295 us

commit v1 on v0

v1 whole, which is shorter than its diff:
```python
import jax
import jax.numpy as jnp
from jax import lax
from jax.experimental import pallas as pl
from jax.experimental.pallas import tpu as pltpu
from jax.sharding import PartitionSpec as P

HI = lax.Precision.HIGHEST
F32 = jnp.float32
N = 64
BLK = 8
SHIFT = 1e-6


def _row(v, k):
    return jnp.broadcast_to(v[k:k + 1, :], (BLK, 2 * N))


def _factor(w):
    w = list(w)
    sub = lax.broadcasted_iota(jnp.int32, (BLK, 2 * N), 0)
    out = []
    for p in range(N // BLK):
        cols = [[jnp.broadcast_to(blk[:, BLK * p + j:BLK * p + j + 1], (BLK, 2 * N)) for j in range(BLK)] for blk in w[p:]]
        row = w[p]
        mults, urows = [], []
        for k in range(BLK):
            inv = 1.0 / _row(cols[0][k], k)
            pivots = [_row(cols[0][j], k) for j in range(k + 1, BLK)]
            urow = _row(row, k)
            mult = [c[k] * inv for c in cols]
            mult[0] = jnp.where(sub > k, mult[0], 0.0)
            for i in range(len(cols)):
                for j in range(k + 1, BLK):
                    cols[i][j] = cols[i][j] - mult[i] * pivots[j - k - 1]
            row = row - mult[0] * urow
            mults.append(mult)
            urows.append(urow)
        for i in range(p + 1, N // BLK):
            for k in range(BLK):
                w[i] = w[i] - mults[k][i - p] * urows[k]
        diag = cols[0][0]
        for k in range(1, BLK):
            diag = jnp.where(sub == k, cols[0][k], diag)
        out.append(row * lax.rsqrt(diag))
    return out


def _factor_kernel(g_ref, o_ref):
    out = _factor([g_ref[BLK * i:BLK * i + BLK, :] for i in range(N // BLK)])
    for i in range(N // BLK):
        o_ref[BLK * i:BLK * i + BLK, :] = out[i]


def _cholesky(gram):
    both = pl.pallas_call(_factor_kernel, out_shape=jax.ShapeDtypeStruct((N, 2 * N), F32))(
        jnp.concatenate([gram, jnp.eye(N, dtype=F32)], axis=1))
    return jnp.triu(both[:, :N]), jnp.tril(both[:, N:])


def _dot(x, y, dims):
    return lax.dot_general(x, y, (dims, ((), ())), precision=HI, preferred_element_type=F32)


def solution(mesh):
    def local_fn(a_blk, b_blk):
        work = a_blk.T
        r_fac = None
        for step in range(3):
            gram = lax.psum(_dot(work, work, ((1,), (1,))), 'rows')
            if step == 0:
                gram = gram + (SHIFT * jnp.trace(gram)) * jnp.eye(N, dtype=F32)
            r_step, inv_t = _cholesky(gram)
            work = _dot(inv_t, work, ((1,), (0,)))
            r_fac = r_step if r_fac is None else _dot(r_step, r_fac, ((1,), (0,)))
        c_mat = lax.psum(_dot(work, b_blk.T, ((1,), (1,))), 'rows')
        return work.T, jnp.triu(r_fac), c_mat

    return jax.shard_map(local_fn, mesh=mesh, in_specs=(P('rows', None), P('rows', None)), out_specs=(P('rows', None), P(), P()), check_vma=False)
```

time: 8800 us -> 189 us (0.02)
  blocking collectives: 6330 us -> 134 us
  other arithmetic: 1150 us -> 2.72 us
  matrix products: 740 us -> 35.2 us
  local copies, waits for them, and re-layouts: 364 us -> 6.04 us
  loops' own time: 177 us -> 0 us
    psum x194 -> x4, blocking collectives: 6330 us -> 134 us  [the longest x3 101 us: local_fn(): gram = lax.psum(_dot(work, work, ((1,), (1,))), 'rows')]
    sub x128 -> x0, other arithmetic: 800 us -> none  [the longest x64 505 us: form_step(): return q_work - (tau_val * reflector)[:, None] * row_proj[None, :]]
    dot_general x129 -> x9, matrix products: 740 us -> 35.2 us  [_dot(): lax.dot_general(x, y, (dims, ((), ())), precision=HI, preferred_element_t...]
    another operation x2 -> x0, loops' own time: 177 us -> none  [the longest x1 176 us: local_fn(): lax.fori_loop(0, num_cols, factor_step, init_state)]
    dynamic_slice x192 -> x0, local copies, waits for them, and re-layouts: 177 us -> none  [the longest x64 69.7 us: factor_step(): column = lax.dynamic_index_in_dim(work_mat, col_idx, axis=1, keepdims=False)]
    mul x130 -> x0, other arithmetic: 124 us -> none  [the longest x64 79.2 us: factor_step(): work_mat = work_mat - (tau_val * reflector)[:, None] * row_proj[None, :]]
    dynamic_update_slice x64 -> x0, local copies, waits for them, and re-layouts: 124 us -> none  [factor_step(): lax.dynamic_update_index_in_dim(reflectors, reflector, col_idx, 0)]
where the time goes in v1:
time: 189 us; the launch traced here: 188 us
  blocking collectives  134 us (71%)
  matrix products  35.2 us (19%)
  Pallas kernels  9.3 us (5%)
  local copies, waits for them, and re-layouts  6.04 us (3%)
  other arithmetic  2.72 us (1%)
    psum x3, blocking collectives, local_fn(): gram = lax.psum(_dot(work, work, ((1,), (1,))), 'rows')  101 us
    dot_general x9, matrix products, _dot(): lax.dot_general(x, y, (dims, ((), ())), precision=HI, preferred_element_t...  35.2 us
    psum x1, blocking collectives, local_fn(): c_mat = lax.psum(_dot(work, b_blk.T, ((1,), (1,))), 'rows')  32.6 us
    pallas_call x3, Pallas kernels, _cholesky(): pl.pallas_call(_factor_kernel, out_shape=jax.ShapeDtypeStruct((N, 2 * N),...  9.3 us
    unnamed x12, local copies, waits for them, and re-layouts  6.04 us

profile of v1, /device:TPU:0, one launch (start us, length us, event | category | flops | bytes accessed | tf_op | source)
XLA Modules:
  0.0 188.2 jit_solution(4535066994235354763)
XLA Ops:
  0.6 0.0 copy-start
  0.6 7.0 %fusion.17 = f32[64,64]{1,0:T(8,128)S(1)} fusion(f32[16384,64]{0,1:T(8,128)} %param.2), kind=kOutput, calls=%fused_computation.33 | convolution fusion | flops 805306368 | bytes 4210688 | tf_op jit(solution)/shard_map/dot_general | solution.py:62
  7.6 34.8 %psum.28 = f32[64,64]{1,0:T(8,128)S(1)} all-reduce(f32[64,64]{1,0:T(8,128)S(1)} %fusion.17), channel_id=1, replica_groups=mesh['rows'=16] {'rows'}, use_global_device_ids=true, to_apply=%region_0.0 | all-reduce | flops 4096 | bytes 32768 | tf_op jit(solution)/shard_map/psum | solution.py:70
  42.5 0.6 select_reduce_fusion
  43.8 0.7 pad_maximum_fusion.g_ref
  44.5 3.1 %shard_map.49 = f32[64,128]{1,0:T(8,128)} custom-call(f32[64,128]{1,0:T(8,128)} %pad_maximum_fusion.g_ref), custom_call_target="tpu_custom_call" | custom-call | tf_op jit(solution)/shard_map/pallas_call | solution.py:56
  47.6 5.4 %fusion.3 = f32[64,16384]{1,0:T(8,128)S(1)} fusion(f32[16384,64]{0,1:T(8,128)} %param.2, f32[64,128]{1,0:T(8,128)} %shard_map.49), kind=kOutput, calls=%fused_computation.10 | convolution fusion | flops 805314560 | bytes 8421376 | tf_op jit(solution)/shard_map/dot_general | solution.py:62
  53.0 0.0 copy-start.2
  53.0 2.0 %copy-done.2 = f32[64,16384]{1,0:T(8,128)} copy-done((f32[64,16384]{1,0:T(8,128)}, f32[64,16384]{1,0:T(8,128)S(1)}, u32[]{:S(2)}) %copy-start.2) | copy-done | bytes 4194328
  55.0 3.4 %fusion.18 = f32[64,64]{1,0:T(8,128)S(1)} fusion(f32[64,16384]{1,0:T(8,128)S(1)} %fusion.3), kind=kOutput, calls=%fused_computation.34 | convolution fusion | flops 805306368 | bytes 4210688 | tf_op jit(solution)/shard_map/dot_general | solution.py:62
  58.4 33.0 %psum.29 = f32[64,64]{1,0:T(8,128)S(1)} all-reduce(f32[64,64]{1,0:T(8,128)S(1)} %fusion.18), channel_id=1, replica_groups=mesh['rows'=16] {'rows'}, use_global_device_ids=true, to_apply=%region_2.3 | all-reduce | flops 4096 | bytes 32768 | tf_op jit(solution)/shard_map/psum | solution.py:70
  91.4 0.7 pad_maximum_fusion.1.g_ref
  92.1 3.1 %shard_map.50 = f32[64,128]{1,0:T(8,128)} custom-call(f32[64,128]{1,0:T(8,128)} %pad_maximum_fusion.1.g_ref), custom_call_target="tpu_custom_call" | custom-call | tf_op jit(solution)/shard_map/pallas_call | solution.py:56
  95.2 5.4 %fusion.2 = f32[64,16384]{1,0:T(8,128)S(1)} fusion(f32[64,16384]{1,0:T(8,128)} %copy-done.2, f32[64,128]{1,0:T(8,128)} %shard_map.50), kind=kOutput, calls=%fused_computation.8 | convolution fusion | flops 805314560 | bytes 8421376 | tf_op jit(solution)/shard_map/dot_general | solution.py:62
  100.6 0.0 copy-start.1
  100.6 2.0 %copy-done.1 = f32[64,16384]{1,0:T(8,128)} copy-done((f32[64,16384]{1,0:T(8,128)}, f32[64,16384]{1,0:T(8,128)S(1)}, u32[]{:S(2)}) %copy-start.1) | copy-done | bytes 4194328
  102.7 0.0 copy-start.4
  102.7 0.0 copy-start.5
  102.7 3.4 %fusion.19 = f32[64,64]{1,0:T(8,128)S(1)} fusion(f32[64,16384]{1,0:T(8,128)S(1)} %fusion.2), kind=kOutput, calls=%fused_computation.35 | convolution fusion | flops 805306368 | bytes 4210688 | tf_op jit(solution)/shard_map/dot_general | solution.py:62
  106.1 33.1 %psum.30 = f32[64,64]{1,0:T(8,128)S(1)} all-reduce(f32[64,64]{1,0:T(8,128)S(1)} %fusion.19), channel_id=1, replica_groups=mesh['rows'=16] {'rows'}, use_global_device_ids=true, to_apply=%region_3.4 | all-reduce | flops 4096 | bytes 32768 | tf_op jit(solution)/shard_map/psum | solution.py:70
  139.1 0.7 pad_maximum_fusion.2.g_ref
  139.8 3.1 %shard_map.51 = f32[64,128]{1,0:T(8,128)} custom-call(f32[64,128]{1,0:T(8,128)} %pad_maximum_fusion.2.g_ref), custom_call_target="tpu_custom_call" | custom-call | tf_op jit(solution)/shard_map/pallas_call | solution.py:56
  142.9 0.0 copy-done.4
  142.9 0.0 copy-done.5
  142.9 0.2 fusion
  143.2 1.6 convolution_select_fusion
  144.8 5.4 %fusion.1 = f32[64,16384]{1,0:T(8,128)S(1)} fusion(f32[64,16384]{1,0:T(8,128)} %copy-done.1, f32[64,128]{1,0:T(8,128)} %shard_map.51), kind=kOutput, calls=%fused_computation.6 | convolution fusion | flops 805314560 | bytes 8421376 | tf_op jit(solution)/shard_map/dot_general | solution.py:62
  150.2 0.0 copy-start.3
  150.2 2.0 %copy-done.3 = f32[64,16384]{1,0:T(8,128)} copy-done((f32[64,16384]{1,0:T(8,128)}, f32[64,16384]{1,0:T(8,128)S(1)}, u32[]{:S(2)}) %copy-start.3) | copy-done | bytes 4194328
  152.2 0.0 copy-done
  152.2 3.4 %fusion.20 = f32[64,4]{0,1:T(4,128)S(1)} fusion(f32[64,16384]{1,0:T(8,128)S(1)} %fusion.1, f32[16384,4]{0,1:T(4,128)S(1)} %copy-done), kind=kOutput, calls=%fused_computation.36 | convolution fusion | flops 50331648 | bytes 4457472 | tf_op jit(solution)/shard_map/dot_general | solution.py:62
  155.6 32.6 %psum.31 = f32[64,4]{0,1:T(4,128)} all-reduce(f32[64,4]{0,1:T(4,128)S(1)} %fusion.20), channel_id=1, replica_groups=mesh['rows'=16] {'rows'}, use_global_device_ids=true, to_apply=%region_4.5 | all-reduce | flops 256 | bytes 2048 | tf_op jit(solution)/shard_map/psum | solution.py:76
  (3 shorter events, 0.0 us)
Async XLA Ops:
  0.6 151.6 %copy-start = (f32[16384,4]{0,1:T(4,128)S(1)}, f32[16384,4]{0,1:T(4,128)}, u32[]{:S(2)}) copy-start(f32[16384,4]{0,1:T(4,128)} %param.3) | copy-start | bytes 786436
  53.0 2.0 %copy-start.2 = (f32[64,16384]{1,0:T(8,128)}, f32[64,16384]{1,0:T(8,128)S(1)}, u32[]{:S(2)}) copy-start(f32[64,16384]{1,0:T(8,128)S(1)} %fusion.3) | copy-start | bytes 12582916
  100.6 2.0 %copy-start.1 = (f32[64,16384]{1,0:T(8,128)}, f32[64,16384]{1,0:T(8,128)S(1)}, u32[]{:S(2)}) copy-start(f32[64,16384]{1,0:T(8,128)S(1)} %fusion.2) | copy-start | bytes 12582916
  102.7 40.3 %copy-start.4 = (f32[64,128]{1,0:T(8,128)S(1)}, f32[64,128]{1,0:T(8,128)}, u32[]{:S(2)}) copy-start(f32[64,128]{1,0:T(8,128)} %shard_map.49) | copy-start | bytes 98308
  102.7 40.3 %copy-start.5 = (f32[64,128]{1,0:T(8,128)S(1)}, f32[64,128]{1,0:T(8,128)}, u32[]{:S(2)}) copy-start(f32[64,128]{1,0:T(8,128)} %shard_map.50) | copy-start | bytes 98308
  150.2 2.0 %copy-start.3 = (f32[64,16384]{1,0:T(8,128)}, f32[64,16384]{1,0:T(8,128)S(1)}, u32[]{:S(2)}) copy-start(f32[64,16384]{1,0:T(8,128)S(1)} %fusion.1) | copy-start | bytes 12582916
